TPU v7x, 512 devices: a whole 4x4x16 slice. The times are simulated.
512 devices in a mesh: rep: 64 (over z, x), shard: 8 (over y, core).
Axes of the slice: x: 4, y: 4, z: 16, core: 2. Of those that a mesh axis runs over, the one named last changes fastest.
Arguments:
- outer_params: float32 [16, 131072], P('shard'), may hold values from -6 to 6
- replica_delta: float32 [64, 16, 131072], P('rep', 'shard'), may hold values from -20 to 20
- momentum: float32 [16, 131072], P('shard', 'rep'), may hold values from -20 to 20
- tensor_of_block: int32 [16], P('shard'), may hold values from 0 to 3, as said below
Outputs:
- new_params: float32 [16, 131072], P('shard')
- new_momentum: float32 [16, 131072], P('shard', 'rep')
Inputs may be any that keep to these rules, and one draw needn't show every extreme that they name: `tensor_of_block`: every tensor owns exactly 4 blocks.
All inputs are finite; a program needn't handle non-finite values.
Results may differ from a plain program's by a relative error of at most 0.00028.
Values sent between devices are 32-bit elements; how exact they have to be, the bound alone decides.
A program may use at most 64 MiB of HBM per device.

v0:
```python
import jax
import jax.numpy as jnp
from jax import lax
from jax.sharding import Mesh
from jax.sharding import PartitionSpec as P

BLOCK_ROWS = 128
BLOCK_COLS = 1024
NS_STEPS = 8
REP = ("rep_0", "rep_1")


outer_rate = 0.7
decay_rate = 0.9


def in_blocks(array, dim, length):
    shape = array.shape
    tiles = array.reshape(*shape[:dim], length, shape[dim] // length, *shape[dim + 1 :])
    return jnp.moveaxis(tiles, dim, 0)


def summed_on_arrival(array, axis, dim):
    length = lax.axis_size(axis)
    tiles = lax.all_to_all(in_blocks(array, dim, length), axis, 0, 0, tiled=True)
    return jnp.sum(tiles, axis=0)


def gathered_by_axis(array, axes, dim):
    if not axes:
        return array
    nearer = lax.all_gather(array, axes[-1], axis=dim, tiled=True)
    return gathered_by_axis(nearer, axes[:-1], dim)


def copy_for_each(array, axis):
    length = lax.axis_size(axis)
    return lax.all_to_all(
        jnp.broadcast_to(array[None], (length, *array.shape)), axis, 0, 0, tiled=True
    )


def over_copies(array, axis):
    return copy_for_each(array, axis).sum(axis=0)


def orthogonalize(direction):
    blocks = direction.reshape(direction.shape[0], BLOCK_ROWS, BLOCK_COLS)
    blocks = blocks / jnp.sqrt(jnp.sum(blocks * blocks, axis=(1, 2), keepdims=True) + 1.0)
    for step in range(NS_STEPS):
        square = jnp.einsum("bij,bkj->bik", blocks, blocks, precision=lax.Precision.HIGHEST)
        blocks = 1.5 * blocks - 0.5 * jnp.einsum(
            "bik,bkj->bij", square, blocks, precision=lax.Precision.HIGHEST
        )
    return blocks.reshape(direction.shape[0], BLOCK_ROWS * BLOCK_COLS)


def group_sums(member, param_part, update_part):
    per_block = jnp.stack(
        [jnp.sum(param_part * param_part, axis=1), jnp.sum(update_part * update_part, axis=1)],
        axis=1,
    )
    return jnp.sum(member[:, :, None] * per_block[:, None, :], axis=0)


def block_rates(tensor_sums, member):
    group_rate = outer_rate * jnp.sqrt(
        jnp.maximum(tensor_sums[:, 0], 1.0) / jnp.maximum(tensor_sums[:, 1], 1.0)
    )
    return jnp.sum(member * group_rate[None, :], axis=1)


def shards(outer_params, replica_delta, momentum, tensor_of_block):
    own_delta = replica_delta[0]
    replicas = lax.axis_size(REP)
    all_blocks = tensor_of_block.shape[0] * lax.axis_size("shard")
    tensors = max(all_blocks // 4, 2)
    member = (tensor_of_block[:, None] == jnp.arange(tensors, dtype=jnp.int32)[None, :]).astype(
        jnp.float32
    )
    owned_delta = summed_on_arrival(own_delta, REP, 1) / replicas
    new_momentum = decay_rate * momentum + owned_delta
    owned_direction = owned_delta + decay_rate * new_momentum
    direction = gathered_by_axis(owned_direction, REP, 1)
    update = orthogonalize(direction)
    tensor_sums = over_copies(group_sums(member, outer_params, update), "shard")
    block_rate = block_rates(tensor_sums, member)
    new_params = outer_params - block_rate[:, None] * update
    return (new_params, new_momentum)


def solution(mesh):
    finer = Mesh(mesh.devices.reshape(16, 4, mesh.shape["shard"]), ("rep_0", "rep_1", "shard"))
    in_specs = (P("shard", None), P(REP, "shard", None), P("shard", REP), P("shard"))
    out_specs = (P("shard", None), P("shard", REP))
    return jax.shard_map(
        shards, mesh=finer, in_specs=in_specs, out_specs=out_specs, check_vma=False
    )
```

profile of v0, /device:TPU:1, one launch (start us, length us, event | category | flops | bytes accessed | tf_op | source)
XLA Modules:
  0.0 198.3 jit_solution(10323035516229591445)
XLA Ops:
  7.2 0.0 all-gather.2.cloned.1.call-start
  7.2 70.7 %all_to_all.10 = f32[64,2,2048]{2,1,0:T(2,128)S(1)} all-to-all(f32[64,2,2048]{2,1,0:T(2,128)} %bitcast.48), channel_id=1, replica_groups=mesh['rep_0'=16,'rep_1'=4,'shard'=8] {'rep_0','rep_1'}, dimensions={0} | all-to-all | bytes 2097152 | tf_op jit(solution)/shard_map/all_to_all | solution.py:25
  77.9 0.0 copy-start.2
  77.9 0.0 copy-start
  77.9 0.4 reduce_sum.64
  78.3 0.4 copy-done.2
  78.7 0.6 multiply_add_fusion
  79.3 12.3 %all_gather.6 = f32[2,8192]{1,0:T(2,128)} all-gather(f32[2,2048]{1,0:T(2,128)S(1)} %get-tuple-element.2), channel_id=1, replica_groups=mesh['rep_0'=16,'rep_1'=4,'shard'=8] {'rep_1'}, dimensions={1}, use_global_device_ids=true | all-gather | bytes 81920 | tf_op jit(solution)/shard_map/all_gather | solution.py:32
  91.6 0.0 all-gather.2.cloned.1.call-update
  91.6 0.0 copy-done
  91.6 0.0 copy-start.3
  91.6 1.2 multiply_reduce_fusion.2
  92.8 0.0 copy-done.3
  92.8 0.1 fusion.9
  92.9 54.7 %all-gather.2.cloned.1.call-done = f32[2,131072]{1,0:T(2,128)} async-done(((f32[2,8192]{1,0:T(2,128)}), f32[2,131072]{1,0:T(2,128)}) %all-gather.2.cloned.1.call-update) | async-done | bytes 1048592 | tf_op jit(solution)/shard_map/all_gather | solution.py:32
  147.6 0.0 copy-start.1
  147.6 2.5 %multiply_reduce_fusion.1 = f32[2]{0:T(128)S(1)} fusion(f32[2,131072]{1,0:T(2,128)} %all-gather.2.cloned.1.call-done), kind=kLoop, calls=%fused_computation.19 | loop fusion | flops 524286 | bytes 1048584 | tf_op jit(solution)/shard_map/reduce_sum | solution.py:49
  150.1 0.0 copy-done.1
  150.1 1.7 fusion.8
  151.8 1.6 fusion.7
  153.4 1.1 fusion.10
  154.5 1.1 fusion.6
  155.5 1.1 fusion.11
  156.6 1.1 fusion.5
  157.7 1.1 fusion.12
  158.8 1.1 fusion.4
  159.9 1.1 fusion.13
  161.0 1.2 fusion.3
  162.2 1.1 fusion.14
  163.3 1.1 fusion.2
  164.4 1.1 fusion.15
  165.5 1.1 fusion.1
  166.5 1.1 fusion.16
  167.6 1.2 multiply_reduce_fusion
  168.9 0.1 copy.8
  169.0 0.1 multiply_reduce_fusion.3
  169.1 0.6 broadcast_in_dim.2
  169.7 15.3 %all-to-all-start.1 = ((f32[8,4,2]{1,2,0:T(2,128)}), f32[8,4,2]{1,2,0:T(2,128)S(1)}, u32[]{:S(2)}, u32[]{:S(2)}) async-start(f32[8,4,2]{1,2,0:T(2,128)} %broadcast_in_dim.2), calls=%async_computation.1 | async-start | bytes 16384 | tf_op jit(solution)/shard_map/all_to_all | solution.py:38
  185.0 0.8 copy.10
  185.8 3.8 %all-to-all-done.1 = f32[8,4,2]{1,2,0:T(2,128)S(1)} async-done(((f32[8,4,2]{1,2,0:T(2,128)}), f32[8,4,2]{1,2,0:T(2,128)S(1)}, u32[]{:S(2)}, u32[]{:S(2)}) %all-to-all-start.1) | async-done | bytes 288 | tf_op jit(solution)/shard_map/all_to_all | solution.py:38
  189.6 0.2 select_reduce_fusion
  189.8 1.6 multiply_subtract_fusion
  (4 shorter events, 0.1 us)
Async XLA Ops:
  7.2 140.4 %all-gather.2.cloned.1.call-start = ((), (), s32[]{:S(2)}) async-start(), calls=%async_computation.2 | async-start | bytes 1114112 | tf_op jit(solution)/shard_map/all_gather | solution.py:32
  77.9 0.7 copy-start.2
  77.9 13.7 %copy-start = (f32[2,131072]{1,0:T(2,128)S(1)}, f32[2,131072]{1,0:T(2,128)}, u32[]{:S(2)}) copy-start(f32[2,131072]{1,0:T(2,128)} %param.4) | copy-start | bytes 3145732
  91.6 1.2 copy-start.3
  147.6 2.5 %copy-start.1 = (f32[2,131072]{1,0:T(2,128)S(1)}, f32[2,131072]{1,0:T(2,128)}, u32[]{:S(2)}) copy-start(f32[2,131072]{1,0:T(2,128)} %all-gather.2.cloned.1.call-done) | copy-start | bytes 3145732
  169.7 19.9 %all-to-all-start.1 = ((f32[8,4,2]{1,2,0:T(2,128)}), f32[8,4,2]{1,2,0:T(2,128)S(1)}, u32[]{:S(2)}, u32[]{:S(2)}) async-start(f32[8,4,2]{1,2,0:T(2,128)} %broadcast_in_dim.2), calls=%async_computation.1 | async-start | bytes 16384 | tf_op jit(solution)/shard_map/all_to_all | solution.py:38
Sparse Core Ops, SparseCore 0:
  91.7 55.8 all-gather.1
where the time goes:
time: 199 us; the launch traced here: 198 us
  blocking collectives  83 us (42%)
  waiting for transfers between devices  58.5 us (29%)
  matrix products  18.6 us (9%)
  starting transfers between devices  15.3 us (8%)
  between operations  14.2 us (7%)
  other arithmetic  6.65 us (3%)
    all_to_all x1, blocking collectives, summed_on_arrival(): lax.all_to_all(in_blocks(array, dim, length), axis, 0, 0, tiled=True)  70.7 us
    all_gather x1, waiting for transfers between devices, gathered_by_axis(): nearer = lax.all_gather(array, axes[-1], axis=dim, tiled=True)  54.7 us
    all_to_all x1, starting transfers between devices, copy_for_each(): lax.all_to_all(jnp.broadcast_to(array[None], (length, *array.shape)), axi...  15.3 us
    all_gather x1, blocking collectives, gathered_by_axis(): nearer = lax.all_gather(array, axes[-1], axis=dim, tiled=True)  12.3 us
    dot_general x8, matrix products, orthogonalize(): jnp.einsum('bij,bkj->bik', blocks, blocks, precision=lax.Precision.HIGHEST)  9.33 us
    dot_general x8, matrix products, orthogonalize(): jnp.einsum('bik,bkj->bij', square, blocks, precision=lax.Precision.HIGHEST)  9.3 us
  transfers between devices with their start and end apart: 2, of which 2 were waited for; matrix products, arithmetic and copies ran while one was open for 1% of the time, Pallas kernels for 0%

commit v1 on v0

v1 whole, which is shorter than its diff:
```python
import jax
import jax.numpy as jnp
from jax import lax
from jax.experimental import pallas as pl
from jax.experimental.pallas import tpu as pltpu
from jax.sharding import Mesh
from jax.sharding import PartitionSpec as P

NZ, NX, NY, NC = 16, 4, 4, 2
CH = 32
HF = CH // 2
ROWS = NZ * NX * CH
NS_STEPS = 8
LEAD = 5
RATE = 0.7
DECAY = 0.9
MESH = pl.DeviceIdType.MESH
HI = lax.Precision.HIGHEST
F32 = jnp.float32

OFFS = [8, 7, -7, 6, -6, 5, -5, 4, -4, 3, -3, 2, -2, 1, -1, 0]
AOFFS = [0, 1, -1, 2, -2, 3, -3, 4, -4, 5, -5, 6, -6, 7, -7, 8]


def kernel(
    tob_ref, params_h, delta_h, mom_h, out_v, newm_v,
    params_v, delta_v, mom_v, dir_v, xm_v,
    ra_v, as_v, rc_v, zs_v, rel_v, zr_v, u_v, sums_v,
    lsem,
    ra_sem, rc_sem, rel_sem, zr_sem, ag_sem, agh_sem, xf_sem, xh_sem, sum_sem,
    sa_sem, sb_sem, sc_sem, sz_sem, sagz_sem, sagzh_sem, sxf_sem, sxh_sem, ssum_sem,
):
    z, x = lax.axis_index("z"), lax.axis_index("x")
    y, c = lax.axis_index("y"), lax.axis_index("core")
    zo = lambda o: lax.rem(z + (o + 2 * NZ), NZ)
    xo = lambda o: lax.rem(x + (o + 2 * NX), NX)
    row = lambda zz, xx, off=0: pl.multiple_of((zz * NX + xx) * CH + off, HF)

    def rdma(src, dst, ssem, rsem, dev):
        return pltpu.make_async_remote_copy(
            src_ref=src, dst_ref=dst, send_sem=ssem, recv_sem=rsem,
            device_id=dev, device_id_type=MESH,
        )

    loads = [
        pltpu.make_async_copy(delta_h, delta_v, lsem.at[0]),
        pltpu.make_async_copy(params_h, params_v, lsem.at[1]),
        pltpu.make_async_copy(mom_h, mom_v, lsem.at[2]),
    ]
    for cp in loads:
        cp.start()

    barrier = pltpu.get_barrier_semaphore()
    count = 0
    for o in (1, -1):
        pl.semaphore_signal(barrier, inc=1, device_id={"x": xo(o)}, device_id_type=MESH)
        count += 1
    for o in (1, -1, 2, -2, 3, -3, 4, -4):
        pl.semaphore_signal(barrier, inc=1, device_id={"z": zo(o)}, device_id_type=MESH)
        count += 1
    shard_peers = []
    for k in range(1, NY * NC):
        me = y * NC + c
        other = lax.rem(me + k, NY * NC)
        shard_peers.append({"y": other // NC, "core": lax.rem(other, NC)})
    for dev in shard_peers:
        pl.semaphore_signal(barrier, inc=1, device_id=dev, device_id_type=MESH)
        count += 1
    loads[0].wait()
    pl.semaphore_wait(barrier, count)

    def send_a(s):
        zd = zo(OFFS[s])
        for d, sg in ((0, 1), (1, -1)):
            src = delta_v.at[pl.ds(row(zd, xo(2), d * HF), HF), :]
            rdma(src, ra_v.at[d, s], sa_sem.at[d], ra_sem.at[d, s], {"x": xo(sg)}).start()

    def send_bc(s):
        zd = zo(OFFS[s])
        for d, sg in ((0, 1), (1, -1)):
            rdma(ra_v.at[d, s], ra_v.at[d, s], sa_sem.at[d], ra_sem.at[d, s], {"x": xo(sg)}).wait_recv()
            own = delta_v[pl.ds(row(zd, xo(sg), d * HF), HF), :]
            as_v[d, s] = own + ra_v[d, s]
        for d, sg in ((0, 1), (1, -1)):
            src = delta_v.at[pl.ds(row(zd, xo(sg), (1 - d) * HF), HF), :]
            dst = rc_v.at[d, s, pl.ds((1 - d) * HF, HF), :]
            rdma(src, dst, sb_sem.at[d], rc_sem.at[d, s], {"x": xo(sg)}).start()
        for d, sg in ((0, 1), (1, -1)):
            dst = rc_v.at[d, s, pl.ds(d * HF, HF), :]
            rdma(as_v.at[d, s], dst, sc_sem.at[d], rc_sem.at[d, s], {"x": xo(sg)}).start()

    def x_total(s):
        zd = zo(OFFS[s])
        for d, sg in ((0, 1), (1, -1)):
            rdma(rc_v.at[d, s], rc_v.at[d, s], sc_sem.at[d], rc_sem.at[d, s], {"x": xo(sg)}).wait_recv()
        return delta_v[pl.ds(row(zd, x), CH), :] + rc_v[0, s] + rc_v[1, s]

    def z_send(s):
        o = OFFS[s]
        t = x_total(s)
        if o == 0:
            zs_v[s] = t
        elif o == 8:
            zs_v[s] = t
            for d, sg in ((0, 1), (1, -1)):
                h = pl.ds(d * HF, HF)
                rdma(zs_v.at[s, h, :], rel_v.at[d, 3, h, :], sz_sem.at[s, d], rel_sem.at[d, 3], {"z": zo(4 * sg)}).start()
        elif abs(o) > 4:
            zs_v[s] = t
            d, sg = (0, 1) if o > 0 else (1, -1)
            k = abs(o) - 4
            rdma(zs_v.at[s], rel_v.at[d, k - 1], sz_sem.at[s, 0], rel_sem.at[d, k - 1], {"z": zo(k * sg)}).start()
        else:
            d, sg = (0, 1) if o > 0 else (1, -1)
            if abs(o) == 4:
                for k in (1, 2, 3):
                    rdma(rel_v.at[d, k - 1], rel_v.at[d, k - 1], sz_sem.at[s, 0], rel_sem.at[d, k - 1], {"z": zo(k * sg)}).wait_recv()
                    t = t + rel_v[d, k - 1]
                h = pl.ds(d * HF, HF)
                rdma(rel_v.at[d, 3, h, :], rel_v.at[d, 3, h, :], sz_sem.at[s, 0], rel_sem.at[d, 3], {"z": zo(4 * sg)}).wait_recv()
                zs_v[s] = t
                zs_v[s, h, :] = zs_v[s, h, :] + rel_v[d, 3, h, :]
            else:
                zs_v[s] = t
            k = abs(o)
            rdma(zs_v.at[s], zr_v.at[d, k - 1], sz_sem.at[s, 0], zr_sem.at[d, k - 1], {"z": zo(k * sg)}).start()

    for s in range(LEAD):
        send_a(s)
    loads[1].wait()
    p2 = []
    for b in range(2):
        part = params_v[pl.ds(b, ROWS // 2, stride=2), :]
        part = jnp.sum((part * part).reshape(ROWS // 16, 8, 128), axis=0)
        p2.append(jnp.sum(jnp.sum(part, axis=0, keepdims=True), axis=1, keepdims=True))
    for s in range(NZ + LEAD):
        if s + LEAD < NZ:
            send_a(s + LEAD)
        if s < NZ:
            send_bc(s)
        if s >= LEAD:
            z_send(s - LEAD)

    total = zs_v[NZ - 1]
    for k in (1, 2, 3, 4):
        for d, sg in ((0, 1), (1, -1)):
            rdma(zr_v.at[d, k - 1], zr_v.at[d, k - 1], sz_sem.at[0, 0], zr_sem.at[d, k - 1], {"z": zo(k * sg)}).wait_recv()
            total = total + zr_v[d, k - 1]
    loads[2].wait()
    mean = total * (1.0 / 64.0)
    newm = DECAY * mom_v[...] + mean
    own = pl.ds(row(z, x), CH)
    dir_v[own, :] = mean + DECAY * newm
    newm_v[...] = newm

    def ag_z(src_o, k, sg, half=None):
        at = row(zo(src_o), x)
        r = pl.ds(at, CH) if half is None else pl.ds(pl.multiple_of(at + half * HF, HF), HF)
        dest_o = (src_o - k * sg + 8) % NZ - 8
        if half is None:
            rsem, ssem = ag_sem.at[dest_o + 8], sagz_sem.at[src_o + 8, (0 if sg > 0 else 1), k - 1]
        else:
            rsem, ssem = agh_sem.at[half], sagzh_sem.at[half]
        ref = dir_v.at[r, :]
        return rdma(ref, ref, ssem, rsem, {"z": zo(k * sg)})

    sends = []

    def go(cp):
        cp.start()
        sends.append(cp)

    for k in (4, 1, 2, 3):
        for sg in (1, -1):
            go(ag_z(0, k, sg))

    def wait_z(o):
        if o == 8:
            for h in range(2):
                ref = dir_v.at[pl.ds(row(zo(8), x, h * HF), HF), :]
                rdma(ref, ref, sagzh_sem.at[h], agh_sem.at[h], {"z": zo(1)}).wait_recv()
        elif o != 0:
            ref = dir_v.at[pl.ds(row(zo(o), x), CH), :]
            rdma(ref, ref, sagzh_sem.at[0], ag_sem.at[(o + 8) % NZ], {"z": zo(1)}).wait_recv()

    def x_first(i):
        o = AOFFS[i]
        wait_z(o)
        if o == -4:
            for k in (4, 3, 2, 1):
                go(ag_z(o, k, 1, 0 if k == 4 else None))
        if o == 4:
            for k in (4, 3, 2, 1):
                go(ag_z(o, k, -1, 1 if k == 4 else None))
        ref = dir_v.at[pl.ds(row(zo(o), x), CH), :]
        for d, sg in ((0, 1), (1, -1)):
            rdma(ref, ref, sxf_sem.at[d], xf_sem.at[d, i], {"x": xo(sg)}).start()

    def x_second(i):
        o = AOFFS[i]
        for d, sg in ((0, 1), (1, -1)):
            ref = dir_v.at[pl.ds(row(zo(o), xo(-sg)), CH), :]
            rdma(ref, ref, sxf_sem.at[d], xf_sem.at[d, i], {"x": xo(sg)}).wait_recv()
            half = dir_v.at[pl.ds(row(zo(o), xo(-sg), d * HF), HF), :]
            rdma(half, half, sxh_sem.at[d], xh_sem.at[d, i], {"x": xo(sg)}).start()

    def relayout(i):
        o = AOFFS[i]
        for d, sg in ((0, 1), (1, -1)):
            half = dir_v.at[pl.ds(row(zo(o), xo(2), d * HF), HF), :]
            rdma(half, half, sxh_sem.at[d], xh_sem.at[d, i], {"x": xo(sg)}).wait_recv()
        base = zo(o) * (NX * CH)
        rows8 = pl.ds(pl.multiple_of(zo(o) * 8, 8), 8)
        for b in range(2):
            for j in range(8):
                xm_v[b, rows8, j * 128 : (j + 1) * 128] = dir_v[pl.ds(base + j * 2 + b, 8, stride=16), :]

    LAG = 3
    for i in range(NZ + 2 * LAG):
        if i < NZ:
            x_first(i)
        if LAG <= i < NZ + LAG:
            x_second(i - LAG)
        if i >= 2 * LAG:
            relayout(i - 2 * LAG)

    r = lax.broadcasted_iota(jnp.int32, (128, 128), 0)
    q = lax.broadcasted_iota(jnp.int32, (128, 128), 1)
    eye = (r == q).astype(F32)

    def all_sum(v):
        return jnp.sum(jnp.sum(v, axis=0, keepdims=True), axis=1, keepdims=True)

    def mm(a, b):
        return jnp.dot(a, b, precision=HI, preferred_element_type=F32)

    grams, scales, prods = [], [], [None, None]
    for b in range(2):
        xb = xm_v[b]
        gram = lax.dot_general(xb, xb, (((1,), (1,)), ((), ())), precision=HI, preferred_element_type=F32)
        norm = all_sum(gram * eye) + 1.0
        grams.append(gram / norm)
        scales.append(lax.rsqrt(norm))
    u2 = [None, None]
    for step in range(NS_STEPS):
        for b in range(2):
            m = 1.5 * eye - 0.5 * grams[b]
            t = mm(grams[b], m)
            prods[b] = m if step == 0 else mm(m, prods[b])
            if step < NS_STEPS - 1:
                grams[b] = mm(t, m)
            else:
                u2[b] = all_sum(t * m)

    rr = lax.broadcasted_iota(jnp.int32, (8, 128), 0)
    qq = lax.broadcasted_iota(jnp.int32, (8, 128), 1)
    tile = jnp.zeros((8, 128), F32)
    for b in range(2):
        mine = rr == tob_ref[b]
        tile = tile + jnp.where(mine & (qq == 0), p2[b], 0.0) + jnp.where(mine & (qq == 1), u2[b], 0.0)
    me = y * NC + c
    sums_v[me] = tile
    for k, dev in enumerate(shard_peers):
        cp = rdma(sums_v.at[me], sums_v.at[me], ssum_sem.at[k], sum_sem.at[6 - k], dev)
        go(cp)
    for b in range(2):
        u_v[b] = mm(prods[b] * scales[b], xm_v[b])
    for k in range(NY * NC - 1):
        other = lax.rem(me + k + 1, NY * NC)
        rdma(sums_v.at[other], sums_v.at[other], ssum_sem.at[k], sum_sem.at[k], shard_peers[k]).wait_recv()
    sums = sums_v[0]
    for k in range(1, NY * NC):
        sums = sums + sums_v[k]
    sums = jnp.maximum(sums, 1.0)
    for b in range(2):
        mine = rr == tob_ref[b]
        num = all_sum(jnp.where(mine & (qq == 0), sums, 0.0))
        den = all_sum(jnp.where(mine & (qq == 1), sums, 0.0))
        rate = RATE * jnp.sqrt(num / den)
        for j in range(8):
            at = pl.ds(j * 2 + b, 128, stride=16)
            out_v[at, :] = params_v[at, :] - rate * u_v[b, :, j * 128 : (j + 1) * 128]

    for d in range(2):
        n = NZ * HF
        for sem in (sa_sem, sb_sem, sc_sem, sxh_sem):
            ref = delta_v.at[pl.ds(0, n), :]
            rdma(ref, ref, sem.at[d], rc_sem.at[d, 0], {"x": xo(1)}).wait_send()
        ref = delta_v.at[pl.ds(0, NZ * CH), :]
        rdma(ref, ref, sxf_sem.at[d], rc_sem.at[d, 0], {"x": xo(1)}).wait_send()
    for s in range(NZ - 1):
        if OFFS[s] == 8:
            for d in range(2):
                h = pl.ds(d * HF, HF)
                rdma(zs_v.at[s, h, :], zs_v.at[s, h, :], sz_sem.at[s, d], rel_sem.at[d, 3], {"z": zo(1)}).wait_send()
        else:
            rdma(zs_v.at[s], zs_v.at[s], sz_sem.at[s, 0], rel_sem.at[0, 0], {"z": zo(1)}).wait_send()
    for cp in sends:
        cp.wait_send()


def shards(outer_params, replica_delta, momentum, tensor_of_block):
    def rows_of(array, blocks=2):
        return array.reshape(blocks, -1, 128).transpose(1, 0, 2).reshape(-1, 128)

    def cols_of(array, blocks=2):
        return array.reshape(-1, blocks, 128).transpose(1, 0, 2).reshape(blocks, -1)

    params, delta, mom = rows_of(outer_params), rows_of(replica_delta[0]), rows_of(momentum)
    dma, vmem = pltpu.SemaphoreType.DMA, pltpu.VMEM
    new_params, new_momentum = pl.pallas_call(
        kernel,
        out_shape=(
            jax.ShapeDtypeStruct(params.shape, F32),
            jax.ShapeDtypeStruct(mom.shape, F32),
        ),
        in_specs=[pl.BlockSpec(memory_space=pltpu.SMEM)] + [pl.BlockSpec(memory_space=pltpu.HBM)] * 3,
        out_specs=[pl.BlockSpec(memory_space=pltpu.VMEM)] * 2,
        scratch_shapes=[
            vmem((ROWS, 128), F32), vmem((ROWS, 128), F32), vmem((CH, 128), F32),
            vmem((ROWS, 128), F32), vmem((2, 128, 1024), F32),
            vmem((2, NZ, HF, 128), F32), vmem((2, NZ, HF, 128), F32), vmem((2, NZ, CH, 128), F32),
            vmem((NZ, CH, 128), F32), vmem((2, 4, CH, 128), F32), vmem((2, 4, CH, 128), F32),
            vmem((2, 128, 1024), F32), vmem((8, 8, 128), F32),
            dma((3,)),
            dma((2, NZ)), dma((2, NZ)), dma((2, 4)), dma((2, 4)), dma((NZ,)), dma((2,)),
            dma((2, NZ)), dma((2, NZ)), dma((7,)),
            dma((2,)), dma((2,)), dma((2,)), dma((NZ, 2)), dma((NZ, 2, 4)), dma((2,)),
            dma((2,)), dma((2,)), dma((7,)),
        ],
        compiler_params=pltpu.CompilerParams(
            collective_id=0, has_side_effects=True, vmem_limit_bytes=40 * 1024 * 1024
        ),
    )(tensor_of_block, params, delta, mom)
    return (cols_of(new_params), cols_of(new_momentum))


def solution(mesh):
    finer = Mesh(mesh.devices.reshape(NZ, NX, NY, NC), ("z", "x", "y", "core"))
    rep, shard = ("z", "x"), ("y", "core")
    in_specs = (P(shard, None), P(rep, shard, None), P(shard, rep), P(shard))
    out_specs = (P(shard, None), P(shard, rep))
    return jax.shard_map(
        shards, mesh=finer, in_specs=in_specs, out_specs=out_specs, check_vma=False
    )
```

time: 199 us -> 79.3 us (0.40)
  blocking collectives: 83 us -> 0 us
  Pallas kernels: 0 us -> 73 us
  waiting for transfers between devices: 58.5 us -> 0 us
  matrix products: 18.6 us -> 0 us
  starting transfers between devices: 15.3 us -> 0 us
  between operations: 14.2 us -> 0.65 us
  other arithmetic: 6.65 us -> 0 us
  local copies, waits for them, and re-layouts: 1.89 us -> 5.39 us
    pallas_call x0 -> x1, Pallas kernels: none -> 73 us  [shards(): pl.pallas_call(kernel, out_shape=(jax.ShapeDtypeStruct(params.shape, F32)...]
    all_to_all x1 -> x0, blocking collectives: 70.7 us -> none  [summed_on_arrival(): lax.all_to_all(in_blocks(array, dim, length), axis, 0, 0, tiled=True)]
    all_gather x1 -> x0, waiting for transfers between devices: 54.7 us -> none  [gathered_by_axis(): nearer = lax.all_gather(array, axes[-1], axis=dim, tiled=True)]
    dot_general x16 -> x0, matrix products: 18.6 us -> none  [the longest x8 9.33 us: orthogonalize(): jnp.einsum('bij,bkj->bik', blocks, blocks, precision=lax.Precision.HIGHEST)]
    all_to_all x1 -> x0, starting transfers between devices: 15.3 us -> none  [copy_for_each(): lax.all_to_all(jnp.broadcast_to(array[None], (length, *array.shape)), axi...]
    all_gather x1 -> x0, blocking collectives: 12.3 us -> none  [gathered_by_axis(): nearer = lax.all_gather(array, axes[-1], axis=dim, tiled=True)]
    reduce_sum x6 -> x0, other arithmetic: 4.33 us -> none  [the longest x1 2.5 us: orthogonalize(): jnp.sum(blocks * blocks, axis=(1, 2), keepdims=True) + 1.0]
    unnamed x9 -> x10, local copies, waits for them, and re-layouts: 1.19 us -> 5.39 us
  transfers between devices with their start and end apart: 2 -> 0, of which waited for: 2 -> 0; matrix products, arithmetic and copies ran while one was open for 1% -> 0% of each run, Pallas kernels for 0% -> 0%
where the time goes in v1:
time: 79.3 us; the launch traced here: 79.1 us
  Pallas kernels  73 us (92%)
  local copies, waits for them, and re-layouts  5.39 us (7%)
    pallas_call x1, Pallas kernels, shards(): pl.pallas_call(kernel, out_shape=(jax.ShapeDtypeStruct(params.shape, F32)...  73 us
    unnamed x10, local copies, waits for them, and re-layouts  5.39 us

profile of v1, /device:TPU:1, one launch (start us, length us, event | category | flops | bytes accessed | tf_op | source)
XLA Modules:
  0.0 79.1 jit_solution(15598887418860777297)
XLA Ops:
  0.6 0.0 copy-start.3
  0.6 0.6 copy-done.3
  1.3 0.0 copy-start
  1.3 1.2 %copy-done = f32[2,131072]{1,0:T(2,128)S(1)} copy-done((f32[2,131072]{1,0:T(2,128)S(1)}, f32[2,131072]{1,0:T(2,128)}, u32[]{:S(2)}) %copy-start) | copy-done | bytes 1048600
  2.5 0.0 copy-start.1
  2.5 1.2 %copy-done.1 = f32[1,2,131072]{2,1,0:T(2,128)S(1)} copy-done((f32[1,2,131072]{2,1,0:T(2,128)S(1)}, f32[1,2,131072]{2,1,0:T(2,128)}, u32[]{:S(2)}) %copy-start.1) | copy-done | bytes 1048600
  3.7 0.0 copy-start.2
  3.7 0.7 copy-done.2
  4.5 73.0 %shard_map.59 = (f32[2048,128]{1,0:T(8,128)S(1)}, f32[32,128]{1,0:T(8,128)S(1)}) custom-call(s32[2]{0:T(128)S(1)} %copy-done.3, f32[2048,128]{1,0:T(8,128)S(1)} %bitcast.25, f32[2048,128]{1,0:T(8,128)S(1)} %bitcast.26, f32[32,128]{1,0:T(8,128)S(1)} %bitcast.28), custom_call_target="tpu_custom_call" | custom-call | tf_op jit(solution)/shard_map/pallas_call | solution.py:311
  77.5 1.0 %copy.13 = f32[2,131072]{1,0:T(2,128)} copy(f32[2,131072]{1,0:T(2,128)S(1)} %bitcast.27) | data formatting | bytes 2097152
  78.5 0.6 copy.14
Async XLA Ops:
  0.6 0.7 copy-start.3
  1.3 1.2 %copy-start = (f32[2,131072]{1,0:T(2,128)S(1)}, f32[2,131072]{1,0:T(2,128)}, u32[]{:S(2)}) copy-start(f32[2,131072]{1,0:T(2,128)} %param.4) | copy-start | bytes 3145732
  2.5 1.2 %copy-start.1 = (f32[1,2,131072]{2,1,0:T(2,128)S(1)}, f32[1,2,131072]{2,1,0:T(2,128)}, u32[]{:S(2)}) copy-start(f32[1,2,131072]{2,1,0:T(2,128)} %param.5) | copy-start | bytes 3145732
  3.7 0.7 copy-start.2
